TPU v7x, 256 devices: a 2x2x32 block of a 4x8x32 slice. The times are simulated.
256 devices in a mesh: groups: 4 (over y, x), ha: 64 (over z, core).
Axes of the slice: x: 2, y: 2, z: 32, core: 2. Of those that a mesh axis runs over, the one named last changes fastest.
The devices are a block of a 4x8x32 slice.
Arguments:
- video: bfloat16 [16, 256, 192, 192], P('groups', 'ha'), parts along dimension 0, may hold values from -6 to 6
- s1_weight: bfloat16 [3, 3, 192, 128], replicated, may hold values from -0.15625 to 0.15625
- t1_weight: bfloat16 [3, 128, 128], replicated, may hold values from -0.3125 to 0.3125
- r1_weight: bfloat16 [2, 2, 128, 256], replicated, may hold values from -0.25 to 0.25
- s2_weight: bfloat16 [3, 3, 256, 256], replicated, may hold values from -0.125 to 0.125
- t2_weight: bfloat16 [3, 256, 256], replicated, may hold values from -0.21875 to 0.21875
- r2_weight: bfloat16 [2, 2, 256, 512], replicated, may hold values from -0.1875 to 0.1875
- attn_gain: bfloat16 [512], replicated, may hold values from 0.5 to 1.5
- w_query: bfloat16 [512, 512], replicated, may hold values from -2.5 to 2.5
- w_key: bfloat16 [512, 512], replicated, may hold values from -0.27 to 0.27
- w_value: bfloat16 [512, 512], replicated, may hold values from -0.25 to 0.25
- w_out: bfloat16 [512, 512], replicated, may hold values from -1 to 1
Outputs:
- encoded: bfloat16 [16, 64, 48, 512], P('groups', 'ha'), parts along dimension 0
There are 4 independent parts, one for each index of `groups`. A program takes and returns all parts, laid end to end along the dimension named above; an argument that names none is the same for every part. Nothing has to cross between parts.
All inputs are finite; a program needn't handle non-finite values.
Results may differ from a plain program's by a relative error of at most 0.018.
Values may be sent and summed in bfloat16 or wider, within the bound.
A program may use at most 128 MiB of HBM per device.

v0:
```python
import math

import jax
import jax.numpy as jnp
from jax import lax
from jax.sharding import PartitionSpec as P


def padded_2(block, sides, width):
    for axis, dim in sides:
        count = lax.axis_size(axis)
        forward = [(i, i + 1) for i in range(count - 1)]
        backward = [(target, source) for source, target in forward]
        low = lax.ppermute(
            lax.slice_in_dim(block, block.shape[dim] - width, None, axis=dim), axis, forward
        )
        high = lax.ppermute(lax.slice_in_dim(block, 0, width, axis=dim), axis, backward)
        block = jnp.concatenate([low, block, high], axis=dim)
    return block


def sent_together(arrays, axis, dim, along):
    ends, at = ([], 0)
    for a in arrays[:-1]:
        at += a.shape[along]
        ends.append(at)
    both = jnp.concatenate(arrays, axis=along)
    return tuple(jnp.split(lax.all_gather(both, axis, axis=dim, tiled=True), ends, axis=along))


def spatial(volume, weight):
    row_count = volume.shape[1] - 2
    col_count = volume.shape[2]
    padded = jnp.pad(volume, ((0, 0), (0, 0), (1, 1), (0, 0)))
    summed = None
    for tap_row in range(3):
        for tap_col in range(3):
            tap_term = jnp.einsum(
                "tywc,co->tywo",
                padded[:, tap_row : tap_row + row_count, tap_col : tap_col + col_count],
                weight[tap_row, tap_col],
                preferred_element_type=jnp.float32,
            )
            summed = tap_term if summed is None else summed + tap_term
    return summed


def temporal(volume, weight):
    frame_count = volume.shape[0]
    padded = jnp.pad(volume, ((2, 0), (0, 0), (0, 0), (0, 0)))
    summed = None
    for tap_time in range(3):
        tap_term = jnp.einsum(
            "tywc,co->tywo",
            padded[tap_time : tap_time + frame_count],
            weight[tap_time],
            preferred_element_type=jnp.float32,
        )
        summed = tap_term if summed is None else summed + tap_term
    return summed


def reduce_pairs(volume, weight):
    frame_count, row_count, col_count, channels = volume.shape
    grouped = volume.reshape(frame_count, row_count // 2, 2, col_count // 2, 2, channels)
    return jnp.einsum("tyixjc,ijco->tyxo", grouped, weight, preferred_element_type=jnp.float32)


def project(normed, weight):
    return jnp.einsum("...c,co->...o", normed, weight, preferred_element_type=jnp.float32).astype(
        jnp.bfloat16
    )


def per_device(
    video,
    s1_weight,
    t1_weight,
    r1_weight,
    s2_weight,
    t2_weight,
    r2_weight,
    attn_gain,
    w_query,
    w_key,
    w_value,
    w_out,
):
    video_rows = padded_2(video, (("ha", 1),), 1)
    a_first = spatial(video_rows, s1_weight).astype(jnp.bfloat16)
    h_first = jax.nn.silu(temporal(a_first, t1_weight)).astype(jnp.bfloat16)
    d_first = reduce_pairs(h_first, r1_weight).astype(jnp.bfloat16)
    middle_halo = padded_2(d_first, (("ha", 1),), 1)
    a_second = spatial(middle_halo, s2_weight).astype(jnp.bfloat16)
    h_second = (d_first.astype(jnp.float32) + jax.nn.silu(temporal(a_second, t2_weight))).astype(
        jnp.bfloat16
    )
    h_third = reduce_pairs(h_second, r2_weight).astype(jnp.bfloat16)
    frame_count, row_count, col_count, channels = h_third.shape
    score_scale = 1.0 / math.sqrt(channels)
    residual = h_third.astype(jnp.float32)
    mean_square = jnp.mean(residual * residual, axis=-1, keepdims=True)
    inverse_norm = lax.rsqrt(mean_square + 1e-06)
    normed = (residual * inverse_norm * attn_gain.astype(jnp.float32)).astype(jnp.bfloat16)
    query_count = row_count * col_count
    queries = project(normed, w_query).reshape(frame_count, query_count, channels)
    key_local = jnp.transpose(project(normed, w_key), (1, 0, 2, 3))
    value_local = jnp.transpose(project(normed, w_value), (1, 0, 2, 3))
    top_score = jnp.full((frame_count, query_count), -1e30, jnp.float32)
    key_piece, value_piece = sent_together((key_local, value_local), "ha", 0, 1)
    scores = (
        jnp.einsum("tqc,rtkc->tqrk", queries, key_piece, preferred_element_type=jnp.float32)
        * score_scale
    )
    scores = scores.reshape(frame_count, query_count, -1)
    new_top = jnp.maximum(top_score, jnp.max(scores, axis=-1))
    weights = jnp.exp(scores - new_top[..., None])
    totals = jnp.sum(weights, axis=-1)
    value_frames = jnp.transpose(value_piece, (1, 0, 2, 3)).reshape(frame_count, -1, channels)
    summed = jnp.einsum(
        "tqk,tkc->tqc",
        weights.astype(jnp.bfloat16),
        value_frames,
        preferred_element_type=jnp.float32,
    )
    top_score, totals, summed = (new_top, totals, summed)
    mixed_rows = (
        (summed / totals[..., None])
        .astype(jnp.bfloat16)
        .reshape(frame_count, row_count, col_count, channels)
    )
    encoded = residual + jnp.einsum(
        "tywc,co->tywo", mixed_rows, w_out, preferred_element_type=jnp.float32
    )
    return encoded.astype(jnp.bfloat16)


def solution(mesh):
    placed = (P("groups", "ha", None, None), P(), P(), P(), P(), P(), P(), P(), P(), P(), P(), P())
    return jax.shard_map(
        per_device,
        mesh=mesh,
        in_specs=placed,
        out_specs=P("groups", "ha", None, None),
        check_vma=False,
    )
```

profile of v0, /device:TPU:37, one launch (start us, length us, event | category | flops | bytes accessed | tf_op | source)
XLA Modules:
  0.0 305.3 jit_solution(13831530059196044943)
XLA Ops:
  6.6 1.3 fusion.135
  7.9 5.1 %collective-permute-start = (bf16[4,1,192,192]{3,2,1,0:T(8,128)(2,1)S(1)}, bf16[4,1,192,192]{3,2,1,0:T(8,128)(2,1)S(1)}, u32[]{:S(2)}, u32[]{:S(2)}) collective-permute-start(bf16[4,1,192,192]{3,2,1,0:T(8,128)(2,1)S(1)} %get-tuple-element.7), channel_id=1, source_target_pairs={{0,1},{1,2},{2,3},{3,4},{4,5},{5,6},{6,7},{7,8},{8,9},{9,10},{10,1... | collective-permute-start | bytes 884744 | tf_op jit(solution)/shard_map/ppermute | solution.py:14
  13.0 18.6 %collective-permute-start.1 = (bf16[4,1,192,192]{3,2,1,0:T(8,128)(2,1)S(1)}, bf16[4,1,192,192]{3,2,1,0:T(8,128)(2,1)S(1)}, u32[]{:S(2)}, u32[]{:S(2)}) collective-permute-start(bf16[4,1,192,192]{3,2,1,0:T(8,128)(2,1)S(1)} %get-tuple-element.8), channel_id=1, source_target_pairs={{1,0},{2,1},{3,2},{4,3},{5,4},{6,5},{7,6},{8,7},{9,8},{10,9},{11,1... | collective-permute-start | bytes 884744 | tf_op jit(solution)/shard_map/ppermute | solution.py:17
  31.6 1.4 fusion.107
  33.0 1.0 fusion.7
  34.5 0.6 fusion.23
  35.7 0.6 fusion.27
  37.3 0.6 fusion.10
  37.9 0.9 add_convert_fusion
  39.6 0.6 multiply_convert_fusion
  40.9 2.1 collective-permute-start.2
  43.0 2.4 collective-permute-start.3
  45.6 4.4 %collective-permute-done.3 = bf16[4,1,96,256]{3,2,1,0:T(8,128)(2,1)S(1)} collective-permute-done((bf16[4,1,96,256]{3,2,1,0:T(8,128)(2,1)S(1)}, bf16[4,1,96,256]{3,2,1,0:T(8,128)(2,1)S(1)}, u32[]{:S(2)}, u32[]{:S(2)}) %collective-permute-start.3) | collective-permute-done | bytes 196640 | tf_op jit(solution)/shard_map/ppermute | solution.py:17
  52.9 0.7 copy-done.7
  55.2 0.7 copy-done.3
  56.6 0.8 pad_maximum_fusion
  57.5 164.7 %all-gather.2.cloned.1.call-done = bf16[64,8,48,512]{3,2,1,0:T(8,128)(2,1)} async-done(((bf16[1,8,48,512]{3,2,1,0:T(8,128)(2,1)}), bf16[64,8,48,512]{3,2,1,0:T(8,128)(2,1)}) %all-gather.2.cloned.1.call-update) | async-done | bytes 25165840 | tf_op jit(solution)/shard_map/all_gather | solution.py:28
  222.2 18.6 %fusion.134 = (bf16[64,4,48,512]{3,2,1,0:T(8,128)(2,1)}, bf16[64,4,48,512]{3,2,1,0:T(8,128)(2,1)}) fusion(bf16[64,8,48,512]{3,2,1,0:T(8,128)(2,1)} %all-gather.2.cloned.1.call-done), kind=kLoop, calls=%fused_computation.157 | loop fusion | bytes 50331648 | tf_op jit(solution)/shard_map/split | solution.py:28
  240.8 22.9 %fusion.137 = (f32[4,48]{1,0:T(4,128)S(1)}, f32[4,48,64,48]{2,1,3,0:T(8,128)}) fusion(bf16[64,4,48,512]{3,2,1,0:T(8,128)(2,1)} %get-tuple-element.5, bf16[4,48,512]{2,1,0:T(8,128)(2,1)S(1)} %multiply_convert_fusion.1, bf16[512,512]{1,0:T(8,128)(2,1)S(1)} %copy-done.11), kind=kOutput, calls=%fused_computation.160 | convolution fusion | flops 705920832 | bytes 15663872 | tf_op jit(solution)/shard_map/tqc,rtkc->tqrk/dot_general | solution.py:112
  263.7 6.3 %copy.26 = f32[4,48,64,48]{3,2,1,0:T(8,128)} copy(f32[4,48,64,48]{2,1,3,0:T(8,128)} %get-tuple-element.14) | data formatting | bytes 4718592 | tf_op jit(solution)/shard_map/mul | solution.py:112
  270.0 3.3 %exponential_reduce_fusion = f32[4,48]{1,0:T(4,128)S(1)} fusion(f32[4,48,64,48]{2,1,3,0:T(8,128)} %get-tuple-element.14, f32[4,48]{1,0:T(4,128)S(1)} %broadcast_maximum_fusion), kind=kLoop, calls=%fused_computation.5 | loop fusion | flops 1179456 | bytes 2360832 | tf_op jit(solution)/shard_map/reduce_sum | solution.py:118
  273.3 6.5 %reshape.65 = f32[4,48,3072]{2,1,0:T(8,128)S(1)} reshape(f32[4,48,64,48]{3,2,1,0:T(8,128)} %copy.26) | data formatting | bytes 4718592 | tf_op jit(solution)/shard_map/reshape | solution.py:115
  279.8 10.7 %copy.58 = bf16[64,4,48,512]{3,2,0,1:T(8,128)(2,1)} copy(bf16[64,4,48,512]{3,2,1,0:T(8,128)(2,1)} %get-tuple-element.6) | data formatting | bytes 25165824
  290.5 8.0 %fusion.40 = bf16[4,1,48,512]{3,2,1,0:T(8,128)(2,1)} fusion(f32[4,48,512]{2,1,0:T(8,128)} %copy-done.3, bf16[4,3072,512]{2,1,0:T(8,128)(2,1)} %bitcast.245, f32[4,48,3072]{2,1,0:T(8,128)S(1)} %reshape.65, f32[4,48]{1,0:T(4,128)S(1)} %broadcast_maximum_fusion, bf16[512,512]{1,0:T(8,128)(2,1)} %param.23, f32[4,48]{1,0:T(4,128)S(1)} %exponential_reduce_fusion), kind=kOutput, calls=%fused_computation.62 | convolution fusion | flops 706215936 | bytes 16057856 | tf_op jit(solution)/shard_map/tywc,co->tywo/dot_general | solution.py:132
  (58 shorter events, 8.7 us)
Async XLA Ops:
  6.5 48.1 %copy-start = (bf16[2,2,256,512]{3,2,1,0:T(8,128)(2,1)S(1)}, bf16[2,2,256,512]{3,2,1,0:T(8,128)(2,1)}, u32[]{:S(2)}) copy-start(bf16[2,2,256,512]{3,2,1,0:T(8,128)(2,1)} %param.18) | copy-start | bytes 3145732
  6.6 25.0 %copy-start.2 = (bf16[4,4,192,192]{3,2,1,0:T(8,128)(2,1)S(1)}, bf16[4,4,192,192]{3,2,1,0:T(8,128)(2,1)}, u32[]{:S(2)}) copy-start(bf16[4,4,192,192]{3,2,1,0:T(8,128)(2,1)} %param.12) | copy-start | bytes 3538948
  6.6 215.7 %all-gather.2.cloned.1.call-start = ((), (), s32[]{:S(2)}) async-start(), calls=%async_computation | async-start | bytes 25559040 | tf_op jit(solution)/shard_map/all_gather | solution.py:28
  7.9 25.1 %collective-permute-start = (bf16[4,1,192,192]{3,2,1,0:T(8,128)(2,1)S(1)}, bf16[4,1,192,192]{3,2,1,0:T(8,128)(2,1)S(1)}, u32[]{:S(2)}, u32[]{:S(2)}) collective-permute-start(bf16[4,1,192,192]{3,2,1,0:T(8,128)(2,1)S(1)} %get-tuple-element.7), channel_id=1, source_target_pairs={{0,1},{1,2},{2,3},{3,4},{4,5},{5,6},{6,7},{7,8},{8,9},{9,10},{10,1... | collective-permute-start | bytes 884744 | tf_op jit(solution)/shard_map/ppermute | solution.py:14
  13.0 20.0 %collective-permute-start.1 = (bf16[4,1,192,192]{3,2,1,0:T(8,128)(2,1)S(1)}, bf16[4,1,192,192]{3,2,1,0:T(8,128)(2,1)S(1)}, u32[]{:S(2)}, u32[]{:S(2)}) collective-permute-start(bf16[4,1,192,192]{3,2,1,0:T(8,128)(2,1)S(1)} %get-tuple-element.8), channel_id=1, source_target_pairs={{1,0},{2,1},{3,2},{4,3},{5,4},{6,5},{7,6},{8,7},{9,8},{10,9},{11,1... | collective-permute-start | bytes 884744 | tf_op jit(solution)/shard_map/ppermute | solution.py:17
  32.9 1.0 copy-start.8
  37.9 0.9 copy-start.9
  39.6 1.0 copy-start.12
  40.2 5.3 %copy-start.10 = (bf16[512]{0:T(512)(128)(2,1)S(1)}, bf16[512]{0:T(512)(128)(2,1)}, u32[]{:S(2)}) copy-start(bf16[512]{0:T(512)(128)(2,1)} %param.19) | copy-start | bytes 3076
  40.9 9.5 %copy-start.4 = (bf16[3,3,256,256]{3,2,1,0:T(8,128)(2,1)S(1)}, bf16[3,3,256,256]{3,2,1,0:T(8,128)(2,1)}, u32[]{:S(2)}) copy-start(bf16[3,3,256,256]{3,2,1,0:T(8,128)(2,1)} %param.16) | copy-start | bytes 3538948
  40.9 4.7 %collective-permute-start.2 = (bf16[4,1,96,256]{3,2,1,0:T(8,128)(2,1)S(1)}, bf16[4,1,96,256]{3,2,1,0:T(8,128)(2,1)S(1)}, u32[]{:S(2)}, u32[]{:S(2)}) collective-permute-start(bf16[4,1,96,256]{3,2,1,0:T(8,128)(2,1)S(1)} %get-tuple-element.9), channel_id=1, source_target_pairs={{0,1},{1,2},{2,3},{3,4},{4,5},{5,6},{6,7},{7,8},{8,9},{9,10},{10,1... | collective-permute-start | bytes 589832 | tf_op jit(solution)/shard_map/ppermute | solution.py:14
  43.0 7.0 %collective-permute-start.3 = (bf16[4,1,96,256]{3,2,1,0:T(8,128)(2,1)S(1)}, bf16[4,1,96,256]{3,2,1,0:T(8,128)(2,1)S(1)}, u32[]{:S(2)}, u32[]{:S(2)}) collective-permute-start(bf16[4,1,96,256]{3,2,1,0:T(8,128)(2,1)S(1)} %get-tuple-element.10), channel_id=1, source_target_pairs={{1,0},{2,1},{3,2},{4,3},{5,4},{6,5},{7,6},{8,7},{9,8},{10,9},{11,1... | collective-permute-start | bytes 589832 | tf_op jit(solution)/shard_map/ppermute | solution.py:17
  52.6 1.0 copy-start.7
  54.5 1.5 copy-start.5
  54.7 1.6 copy-start.6
  55.2 0.8 copy-start.3
  57.5 183.4 %copy-start.11 = (bf16[512,512]{1,0:T(8,128)(2,1)S(1)}, bf16[512,512]{1,0:T(8,128)(2,1)}, u32[]{:S(2)}) copy-start(bf16[512,512]{1,0:T(8,128)(2,1)} %param.20) | copy-start | bytes 1572868
  290.5 8.0 %copy-start.1 = (bf16[2,2,256,512]{3,2,1,0:T(8,128)(2,1)S(1)}, bf16[2,2,256,512]{3,2,1,0:T(8,128)(2,1)}, u32[]{:S(2)}) copy-start(bf16[2,2,256,512]{3,2,1,0:T(8,128)(2,1)} %param.18) | copy-start | bytes 3145732
Sparse Core Ops, SparseCore 0:
  57.6 164.5 all-gather.1
where the time goes:
time: 306 us; the launch traced here: 305 us
  waiting for transfers between devices  169 us (55%)
  local copies, waits for them, and re-layouts  45.4 us (15%)
  matrix products  43 us (14%)
  starting transfers between devices  28.2 us (9%)
  between operations  13.8 us (5%)
  other arithmetic  5.44 us (2%)
    all_gather x1, waiting for transfers between devices, sent_together(): lax.all_gather(both, axis, axis=dim, tiled=True)  165 us
    dot_general x1, matrix products, per_device(): jnp.einsum('tqc,rtkc->tqrk', queries, key_piece, preferred_element_type=j...  22.9 us
    ppermute x2, starting transfers between devices, padded_2(): lax.ppermute(lax.slice_in_dim(block, 0, width, axis=dim), axis, backward)  21 us
    split x1, local copies, waits for them, and re-layouts, sent_together(): jnp.split(lax.all_gather(both, axis, axis=dim, tiled=True), ends, axis=al...  18.6 us
    unnamed x27, local copies, waits for them, and re-layouts  12.5 us
    dot_general x18, matrix products, spatial(): jnp.einsum('tywc,co->tywo', padded[:, tap_row:tap_row + row_count, tap_co...  8.6 us
    dot_general x1, matrix products, per_device(): jnp.einsum('tywc,co->tywo', mixed_rows, w_out, preferred_element_type=jnp...  7.98 us
    ppermute x2, starting transfers between devices, padded_2(): lax.ppermute(lax.slice_in_dim(block, block.shape[dim] - width, None, axis...  7.17 us
  transfers between devices with their start and end apart: 5, of which 3 were waited for; matrix products, arithmetic and copies ran while one was open for 0% of the time, Pallas kernels for 0%

commit v1 on v0

v1 whole, which is shorter than its diff:
```python
import functools
import math

import jax
import jax.numpy as jnp
from jax import lax
from jax.experimental import pallas as pl
from jax.experimental.pallas import tpu as pltpu
from jax.sharding import PartitionSpec as P

F32 = jnp.float32
BF16 = jnp.bfloat16


def silu(x):
    return x / (1.0 + jnp.exp(-x))


def side_sum(acc, width, period):
    rows = acc.shape[0]
    site = lax.rem(lax.broadcasted_iota(jnp.int32, (rows, width), 0), period)
    low = pltpu.roll(acc[:, :width], 1, 0)
    high = pltpu.roll(acc[:, 2 * width :], rows - 1, 0)
    low = jnp.where(site == 0, 0.0, low)
    high = jnp.where(site == period - 1, 0.0, high)
    return acc[:, width : 2 * width] + low + high


def kernel(
    n,
    video,
    s1,
    t1,
    r1,
    s2,
    t2,
    r2,
    gain,
    wq,
    wk,
    wv,
    wo,
    out,
    vp,
    w1,
    t1v,
    r1v,
    w2,
    t2v,
    r2v,
    gainv,
    wqv,
    wkv,
    wvv,
    wov,
    a1p,
    h1s,
    d1p,
    a2p,
    h2s,
    res,
    keys,
    qp,
    top,
    total,
    mixed,
    video_sem,
    w1_sem,
    w2_sem,
    weight_sem,
    halo1_send,
    halo1_recv,
    halo2_send,
    halo2_recv,
    own_send,
    own_recv,
    ring_send,
    ring_recv,
    pair_send,
    pair_recv,
    last_send,
):
    frames, rows, width, _ = video.shape
    c1 = t1.shape[1]
    c2 = t2.shape[1]
    c3 = wq.shape[0]
    half_rows, half_width = rows // 2, width // 2
    sites = out.shape[1] * out.shape[2]
    half = frames // 2
    hops = n // 4

    ha = lax.axis_index("ha")
    core = lax.rem(ha, 2)
    up = lax.rem(ha + n - 1, n)
    down = lax.rem(ha + 1, n)
    partner = ha + 1 - 2 * core
    after = lax.rem(ha + n + 2 - 4 * core, n)
    two_up = lax.rem(ha + n - 2, n)
    two_down = lax.rem(ha + 2, n)

    def video_copy(t):
        return pltpu.make_async_copy(video.at[t], vp.at[t, pl.ds(1, rows)], video_sem.at[t])

    def w1_copy(i, j):
        return pltpu.make_async_copy(
            s1.at[i, j], w1.at[i, :, pl.ds(j * c1, c1)], w1_sem.at[i, j]
        )

    def w2_copy(i, j):
        return pltpu.make_async_copy(
            s2.at[i, j], w2.at[i, :, pl.ds(j * c2, c2)], w2_sem.at[i, j]
        )

    plain = ((t1, t1v), (r1, r1v), (t2, t2v), (r2, r2v), (gain, gainv), (wq, wqv), (wk, wkv), (wv, wvv), (wo, wov))

    def plain_copy(k):
        return pltpu.make_async_copy(plain[k][0], plain[k][1], weight_sem.at[k])

    for i in range(3):
        for j in range(3):
            w1_copy(i, j).start()
    for t in range(frames):
        video_copy(t).start()
    for k in range(2):
        plain_copy(k).start()

    barrier = pltpu.get_barrier_semaphore()
    for other in (up, down, two_up, two_down):
        pl.semaphore_signal(
            barrier, inc=1, device_id={"ha": other}, device_id_type=pl.DeviceIdType.MESH
        )
    pl.semaphore_wait(barrier, 4)

    def remote(src, dst, send, recv, to):
        return pltpu.make_async_remote_copy(
            src_ref=src,
            dst_ref=dst,
            send_sem=send,
            recv_sem=recv,
            device_id={"ha": to},
            device_id_type=pl.DeviceIdType.MESH,
        )

    def halo1(d, t):
        if d == 0:
            src, dst, to = video.at[t, rows - 1], vp.at[t, 0], down
        else:
            src, dst, to = video.at[t, 0], vp.at[t, rows + 1], up
        return remote(src, dst, halo1_send.at[d, t], halo1_recv.at[d, t], to)

    def halo2(d, t):
        if d == 0:
            src, dst, to = d1p.at[t, half_rows], d1p.at[t, 0], down
        else:
            src, dst, to = d1p.at[t, 1], d1p.at[t, half_rows + 1], up
        return remote(src, dst, halo2_send.at[d, t], halo2_recv.at[d, t], to)

    for t in range(frames):
        halo1(0, t).start()
        halo1(1, t).start()

    for i in range(3):
        for j in range(3):
            w2_copy(i, j).start()
    for k in range(2, len(plain)):
        plain_copy(k).start()

    a1p[0:2] = jnp.zeros((2,) + a1p.shape[1:], BF16)
    a2p[0:2] = jnp.zeros((2,) + a2p.shape[1:], BF16)

    for i in range(3):
        for j in range(3):
            w1_copy(i, j).wait()

    def first_row(t, y):
        acc = None
        for i in range(3):
            term = jnp.dot(vp[t, y + i], w1[i], preferred_element_type=F32)
            acc = term if acc is None else acc + term
        a1p[t + 2, y] = side_sum(acc, c1, width).astype(BF16)

    def inner_rows(t, carry):
        video_copy(t).wait()
        for y in range(1, rows - 1):
            first_row(t, y)
        return carry

    lax.fori_loop(0, frames, inner_rows, 0)

    plain_copy(0).wait()
    plain_copy(1).wait()

    def first_level(t):
        halo1(0, t).wait_recv()
        halo1(1, t).wait_recv()

        @pl.when(ha == 0)
        def _():
            vp[t, 0] = jnp.zeros(vp.shape[2:], BF16)

        @pl.when(ha == n - 1)
        def _():
            vp[t, rows + 1] = jnp.zeros(vp.shape[2:], BF16)

        first_row(t, 0)
        first_row(t, rows - 1)
        for y in range(rows):
            stack = jnp.concatenate([a1p[t, y], a1p[t + 1, y], a1p[t + 2, y]], axis=1)
            h1s[y] = silu(jnp.dot(stack, t1v[...], preferred_element_type=F32))
        for y in range(half_rows):
            parts = [
                h1s[2 * y + i, pl.ds(j, half_width, stride=2), :].astype(BF16)
                for i in range(2)
                for j in range(2)
            ]
            d = jnp.dot(jnp.concatenate(parts, axis=1), r1v[...], preferred_element_type=F32)
            d1p[t, y + 1] = d.astype(BF16)
        halo2(0, t).start()
        halo2(1, t).start()

    for t in range(frames):
        first_level(t)

    for i in range(3):
        for j in range(3):
            w2_copy(i, j).wait()
    for k in (2, 3, 4):
        plain_copy(k).wait()

    def own_copy(t):
        return remote(
            keys.at[t, 0, 0, core], keys.at[t, 0, 0, core], own_send.at[t], own_recv.at[t], partner
        )

    def ring_copy(s, f):
        if isinstance(s, int) and s == 0:
            src, dst = keys.at[f, 0, 0], keys.at[f, 1, core]
        elif isinstance(s, int) and s == hops - 1:
            src, dst = keys.at[f, s, core], keys.at[f, 0, 1]
        else:
            src, dst = keys.at[f, s, core], keys.at[f, s + 1, core]
        return remote(
            src, dst, ring_send.at[lax.rem(s, 2), f], ring_recv.at[s + 1, f], after
        )

    def pair_copy(s, f):
        ref = keys.at[f, s, core]
        return remote(ref, ref, pair_send.at[lax.rem(s, 2), f], pair_recv.at[s, f], partner)

    def last_copy(f):
        ref = keys.at[f, 0, 1]
        return remote(ref, ref, last_send.at[lax.rem(f, half)], pair_recv.at[hops, f], partner)

    def second_level(t):
        halo2(0, t).wait_recv()
        halo2(1, t).wait_recv()

        @pl.when(ha == 0)
        def _():
            d1p[t, 0] = jnp.zeros(d1p.shape[2:], BF16)

        @pl.when(ha == n - 1)
        def _():
            d1p[t, half_rows + 1] = jnp.zeros(d1p.shape[2:], BF16)

        count = half_rows * half_width
        acc = None
        for i in range(3):
            block = d1p[t, i : i + half_rows].reshape(count, c2)
            term = jnp.dot(block, w2[i], preferred_element_type=F32)
            acc = term if acc is None else acc + term
        a2p[t + 2] = side_sum(acc, c2, half_width).astype(BF16)
        stack = jnp.concatenate([a2p[t], a2p[t + 1], a2p[t + 2]], axis=1)
        mid = silu(jnp.dot(stack, t2v[...], preferred_element_type=F32))
        mid = mid + d1p[t, 1 : half_rows + 1].reshape(count, c2).astype(F32)
        for b in range(c2 // 128):
            h2s[b] = mid[:, b * 128 : (b + 1) * 128]
        parts = [
            h2s[b, pl.ds(i * half_width + j, sites, stride=2), :].astype(BF16)
            for i in range(2)
            for j in range(2)
            for b in range(c2 // 128)
        ]
        h3 = jnp.dot(jnp.concatenate(parts, axis=1), r2v[...], preferred_element_type=F32)
        h3 = h3.astype(BF16).astype(F32)
        res[t] = h3
        mean_square = jnp.mean(h3 * h3, axis=-1, keepdims=True)
        normed = h3 * lax.rsqrt(mean_square + 1e-06) * gainv[...].astype(F32)
        keys[t, 0, 0, core] = normed.astype(BF16)
        own_copy(t).start()

        if t > 0:
            own_copy(t - 1).wait_recv()
            ring_copy(0, t - 1).start()

    for t in range(frames):
        second_level(t)

    own_copy(frames - 1).wait_recv()
    ring_copy(0, frames - 1).start()

    plain_copy(5).wait()
    plain_copy(6).wait()
    normed = keys[:, 0, 0, core].reshape(frames * sites, c3)
    queries = jnp.dot(normed, wqv[...], preferred_element_type=F32).astype(BF16)
    mapped = lax.dot_general(
        queries, wkv[...], (((1,), (1,)), ((), ())), preferred_element_type=F32
    )
    mapped = (mapped * (1.0 / math.sqrt(c3))).astype(BF16)
    qp[...] = mapped.reshape(frames, sites, c3)
    top[...] = jnp.full(top.shape, -1e30, F32)
    total[...] = jnp.zeros(total.shape, F32)
    mixed[...] = jnp.zeros(mixed.shape, F32)

    def attend(s, f):
        block = keys[f, s].reshape(4 * sites, c3)
        scores = lax.dot_general(
            qp[f], block, (((1,), (1,)), ((), ())), preferred_element_type=F32
        )
        old = top[f]
        new = jnp.maximum(old, jnp.max(scores, axis=-1, keepdims=True))
        decay = jnp.exp(old - new)
        weights = jnp.exp(scores - new[:, :1])
        total[f] = total[f] * decay + jnp.sum(weights, axis=-1, keepdims=True)
        mixed[f] = mixed[f] * decay[:, :1] + jnp.dot(
            weights.astype(BF16), block, preferred_element_type=F32
        )
        top[f] = new

    def hop(s, carry):
        for f in range(frames):
            receive_from = remote(
                keys.at[f, s, core],
                keys.at[f, s, core],
                ring_send.at[lax.rem(s, 2), f],
                ring_recv.at[s, f],
                after,
            )
            receive_from.wait_recv()

            @pl.when(s >= 2)
            def _():
                ring_copy(s - 2, f).wait_send()

            ring_copy(s, f).start()

            @pl.when(s >= 3)
            def _():
                pair_copy(s - 2, f).wait_send()

            pair_copy(s, f).start()

            @pl.when(s >= 2)
            def _():
                pair_copy(s - 1, f).wait_recv()
                attend(s - 1, f)

        return carry

    lax.fori_loop(1, hops - 1, hop, 0)

    end = hops - 1
    for f in range(frames):
        ring_copy(end - 1, f).wait_recv()
        ring_copy(end - 2, f).wait_send()

        @pl.when(core == f // half)
        def _():
            ring_copy(end, f).start()

        pair_copy(end - 2, f).wait_send()
        pair_copy(end, f).start()
        pair_copy(end - 1, f).wait_recv()
        attend(end - 1, f)

    for f in range(frames):
        @pl.when(core == f // half)
        def _():
            ring_copy(end, f).wait_recv()
            last_copy(f).start()

        pair_copy(end, f).wait_recv()
        attend(end, f)

    for k in (7, 8):
        plain_copy(k).wait()
    for f in range(frames):
        @pl.when(core != f // half)
        def _():
            last_copy(f).wait_recv()

        attend(0, f)

    mean = jnp.concatenate([mixed[f] / total[f][:, :1] for f in range(frames)], axis=0)
    values = jnp.dot(mean.astype(BF16), wvv[...], preferred_element_type=F32).astype(BF16)
    encoded = res[...].reshape(frames * sites, c3) + jnp.dot(
        values, wov[...], preferred_element_type=F32
    )
    out[...] = encoded.astype(BF16).reshape(out.shape)

    for t in range(frames):
        for d in range(2):
            halo1(d, t).wait_send()
            halo2(d, t).wait_send()
        own_copy(t).wait_send()
        ring_copy(end - 1, t).wait_send()
        pair_copy(end - 1, t).wait_send()
        pair_copy(end, t).wait_send()

        @pl.when(core == t // half)
        def _():
            ring_copy(end, t).wait_send()
            last_copy(t).wait_send()


def per_device(n, video, s1, t1, r1, s2, t2, r2, gain, wq, wk, wv, wo):
    frames, rows, width, c0 = video.shape
    c1, c2, c3 = t1.shape[1], t2.shape[1], wq.shape[0]
    half_rows, half_width = rows // 2, width // 2
    sites = (half_rows // 2) * (half_width // 2)
    hops = n // 4
    dma = pltpu.SemaphoreType.DMA
    scratch = [
        pltpu.VMEM((frames, rows + 2, width, c0), BF16),
        pltpu.VMEM((3, c0, 3 * c1), BF16),
        pltpu.VMEM((3 * c1, c1), BF16),
        pltpu.VMEM((4 * c1, c2), BF16),
        pltpu.VMEM((3, c2, 3 * c2), BF16),
        pltpu.VMEM((3 * c2, c2), BF16),
        pltpu.VMEM((4 * c2, c3), BF16),
        pltpu.VMEM((1, c3), BF16),
        pltpu.VMEM((c3, c3), BF16),
        pltpu.VMEM((c3, c3), BF16),
        pltpu.VMEM((c3, c3), BF16),
        pltpu.VMEM((c3, c3), BF16),
        pltpu.VMEM((frames + 2, rows, width, c1), BF16),
        pltpu.VMEM((rows, width, c1), F32),
        pltpu.VMEM((frames, half_rows + 2, half_width, c2), BF16),
        pltpu.VMEM((frames + 2, half_rows * half_width, c2), BF16),
        pltpu.VMEM((c2 // 128, half_rows * half_width, 128), F32),
        pltpu.VMEM((frames, sites, c3), F32),
        pltpu.VMEM((frames, hops, 2, 2, sites, c3), BF16),
        pltpu.VMEM((frames, sites, c3), BF16),
        pltpu.VMEM((frames, sites, 128), F32),
        pltpu.VMEM((frames, sites, 128), F32),
        pltpu.VMEM((frames, sites, c3), F32),
        dma((frames,)),
        dma((3, 3)),
        dma((3, 3)),
        dma((9,)),
        dma((2, frames)),
        dma((2, frames)),
        dma((2, frames)),
        dma((2, frames)),
        dma((frames,)),
        dma((frames,)),
        dma((2, frames)),
        dma((hops + 1, frames)),
        dma((2, frames)),
        dma((hops + 1, frames)),
        dma((frames // 2,)),
    ]
    out = pl.pallas_call(
        functools.partial(kernel, n),
        out_shape=jax.ShapeDtypeStruct((frames, half_rows // 2, half_width // 2, c3), BF16),
        in_specs=[pl.BlockSpec(memory_space=pl.ANY)] * 12,
        out_specs=pl.BlockSpec(memory_space=pltpu.VMEM),
        scratch_shapes=scratch,
        compiler_params=pltpu.CompilerParams(
            collective_id=0, has_side_effects=True, vmem_limit_bytes=60 * 1024 * 1024
        ),
        name="encoder",
    )(
        video,
        s1,
        t1.reshape(3 * c1, c1),
        r1.reshape(4 * c1, c2),
        s2,
        t2.reshape(3 * c2, c2),
        r2.reshape(4 * c2, c3),
        gain.reshape(1, c3),
        wq,
        wk,
        wv,
        wo,
    )
    return out


def solution(mesh):
    placed = (P("groups", "ha", None, None),) + (P(),) * 11
    return jax.shard_map(
        functools.partial(per_device, mesh.shape["ha"]),
        mesh=mesh,
        in_specs=placed,
        out_specs=P("groups", "ha", None, None),
        check_vma=False,
    )
```

time: 306 us -> 111 us (0.36)
  waiting for transfers between devices: 169 us -> 0 us
  Pallas kernels: 0 us -> 108 us
  matrix products: 43 us -> 0 us
  local copies, waits for them, and re-layouts: 45.4 us -> 2.88 us
  starting transfers between devices: 28.2 us -> 0 us
  between operations: 13.8 us -> 0.01 us
  other arithmetic: 5.44 us -> 0 us
    all_gather x1 -> x0, waiting for transfers between devices: 165 us -> none  [sent_together(): lax.all_gather(both, axis, axis=dim, tiled=True)]
    pallas_call x0 -> x1, Pallas kernels: none -> 108 us  [per_device(): pl.pallas_call(functools.partial(kernel, n), out_shape=jax.ShapeDtypeStru...]
    dot_general x30 -> x0, matrix products: 43 us -> none  [the longest x1 22.9 us: per_device(): jnp.einsum('tqc,rtkc->tqrk', queries, key_piece, preferred_element_type=j...]
    ppermute x4 -> x0, starting transfers between devices: 28.2 us -> none  [the longest x2 21 us: padded_2(): lax.ppermute(lax.slice_in_dim(block, 0, width, axis=dim), axis, backward)]
    split x1 -> x0, local copies, waits for them, and re-layouts: 18.6 us -> none  [sent_together(): jnp.split(lax.all_gather(both, axis, axis=dim, tiled=True), ends, axis=al...]
    unnamed x27 -> x1, local copies, waits for them, and re-layouts: 12.5 us -> 1.62 us
    mul x1 -> x0, local copies, waits for them, and re-layouts: 6.31 us -> none  [per_device(): jnp.einsum('tqc,rtkc->tqrk', queries, key_piece, preferred_element_type=j...]
    reshape x2 -> x1, local copies, waits for them, and re-layouts: 6.62 us -> 1.26 us  [per_device(): gain.reshape(1, c3)]
  transfers between devices with their start and end apart: 5 -> 0, of which waited for: 3 -> 0; matrix products, arithmetic and copies ran while one was open for 0% -> 0% of each run, Pallas kernels for 0% -> 0%
where the time goes in v1:
time: 111 us
  Pallas kernels  108 us (97%)
  local copies, waits for them, and re-layouts  2.88 us (3%)
    pallas_call x1, Pallas kernels, per_device(): pl.pallas_call(functools.partial(kernel, n), out_shape=jax.ShapeDtypeStru...  108 us

profile of v1, /device:TPU:37, one launch (start us, length us, event | category | flops | bytes accessed | tf_op | source)
XLA Modules:
  0.0 111.3 jit_solution(18041657594701839351)
XLA Ops:
  0.0 1.3 %reshape.19.gain = bf16[1,512]{1,0:T(2,128)(2,1)} reshape(bf16[512]{0:T(512)(128)(2,1)} %param.19) | data formatting | bytes 2048 | tf_op jit(solution)/shard_map/reshape | solution.py:481
  1.3 108.4 %encoder.1 = bf16[4,1,48,512]{3,2,1,0:T(8,128)(2,1)} custom-call(bf16[4,4,192,192]{3,2,1,0:T(8,128)(2,1)} %video.1, bf16[3,3,192,128]{3,2,1,0:T(8,128)(2,1)} %s1_.1, bf16[384,128]{1,0:T(8,128)(2,1)} %bitcast.7, bf16[512,256]{1,0:T(8,128)(2,1)} %bitcast.6, bf16[3,3,256,256]{3,2,1,0:T(8,128)(2,1)} %s2_.1, bf16[768,256]{1,0:T(8,128)(2,1)} %bitcast.5, ...), custom_call_target="tpu_custom_call" | custom-call | tf_op jit(solution)/shard_map/encoder/pallas_call | solution.py:463
  109.7 1.6 %copy.14 = bf16[4,1,48,512]{3,2,1,0:T(8,128)(2,1)} copy(bf16[4,1,48,512]{3,2,1,0:T(8,128)(2,1)} %encoder.1) | data formatting | bytes 393216

commit v2 on v1

--- a/solution.py
+++ b/solution.py
@@ -98,38 +98,37 @@
     two_up = lax.rem(ha + n - 2, n)
     two_down = lax.rem(ha + 2, n)
 
-    def video_copy(t):
-        return pltpu.make_async_copy(video.at[t], vp.at[t, pl.ds(1, rows)], video_sem.at[t])
-
-    def w1_copy(i, j):
-        return pltpu.make_async_copy(
-            s1.at[i, j], w1.at[i, :, pl.ds(j * c1, c1)], w1_sem.at[i, j]
-        )
-
-    def w2_copy(i, j):
-        return pltpu.make_async_copy(
-            s2.at[i, j], w2.at[i, :, pl.ds(j * c2, c2)], w2_sem.at[i, j]
-        )
-
-    plain = ((t1, t1v), (r1, r1v), (t2, t2v), (r2, r2v), (gain, gainv), (wq, wqv), (wk, wkv), (wv, wvv), (wo, wov))
-
-    def plain_copy(k):
-        return pltpu.make_async_copy(plain[k][0], plain[k][1], weight_sem.at[k])
-
-    for i in range(3):
-        for j in range(3):
-            w1_copy(i, j).start()
-    for t in range(frames):
-        video_copy(t).start()
-    for k in range(2):
-        plain_copy(k).start()
-
     barrier = pltpu.get_barrier_semaphore()
     for other in (up, down, two_up, two_down):
         pl.semaphore_signal(
             barrier, inc=1, device_id={"ha": other}, device_id_type=pl.DeviceIdType.MESH
         )
-    pl.semaphore_wait(barrier, 4)
+
+    def video_copy(t):
+        return pltpu.make_async_copy(video.at[t], vp.at[t, pl.ds(1, rows)], video_sem.at[t])
+
+    def w1_copy(i, j):
+        return pltpu.make_async_copy(
+            s1.at[i, j], w1.at[i, :, pl.ds(j * c1, c1)], w1_sem.at[i, j]
+        )
+
+    def w2_copy(i, j):
+        return pltpu.make_async_copy(
+            s2.at[i, j], w2.at[i, :, pl.ds(j * c2, c2)], w2_sem.at[i, j]
+        )
+
+    plain = ((t1, t1v), (r1, r1v), (t2, t2v), (r2, r2v), (gain, gainv), (wq, wqv), (wk, wkv), (wv, wvv), (wo, wov))
+
+    def plain_copy(k):
+        return pltpu.make_async_copy(plain[k][0], plain[k][1], weight_sem.at[k])
+
+    for t in range(frames):
+        video_copy(t).start()
+    for i in range(3):
+        for j in range(3):
+            w1_copy(i, j).start()
+    for k in range(2):
+        plain_copy(k).start()
 
     def remote(src, dst, send, recv, to):
         return pltpu.make_async_remote_copy(
@@ -143,9 +142,9 @@
 
     def halo1(d, t):
         if d == 0:
-            src, dst, to = video.at[t, rows - 1], vp.at[t, 0], down
+            src, dst, to = vp.at[t, rows], vp.at[t, 0], down
         else:
-            src, dst, to = video.at[t, 0], vp.at[t, rows + 1], up
+            src, dst, to = vp.at[t, 1], vp.at[t, rows + 1], up
         return remote(src, dst, halo1_send.at[d, t], halo1_recv.at[d, t], to)
 
     def halo2(d, t):
@@ -155,7 +154,12 @@
             src, dst, to = d1p.at[t, 1], d1p.at[t, half_rows + 1], up
         return remote(src, dst, halo2_send.at[d, t], halo2_recv.at[d, t], to)
 
+    a1p[0:2] = jnp.zeros((2,) + a1p.shape[1:], BF16)
+    a2p[0:2] = jnp.zeros((2,) + a2p.shape[1:], BF16)
+
+    pl.semaphore_wait(barrier, 4)
     for t in range(frames):
+        video_copy(t).wait()
         halo1(0, t).start()
         halo1(1, t).start()
 
@@ -164,9 +168,6 @@
             w2_copy(i, j).start()
     for k in range(2, len(plain)):
         plain_copy(k).start()
-
-    a1p[0:2] = jnp.zeros((2,) + a1p.shape[1:], BF16)
-    a2p[0:2] = jnp.zeros((2,) + a2p.shape[1:], BF16)
 
     for i in range(3):
         for j in range(3):
@@ -180,7 +181,6 @@
         a1p[t + 2, y] = side_sum(acc, c1, width).astype(BF16)
 
     def inner_rows(t, carry):
-        video_copy(t).wait()
         for y in range(1, rows - 1):
             first_row(t, y)
         return carry
@@ -217,15 +217,6 @@
             d1p[t, y + 1] = d.astype(BF16)
         halo2(0, t).start()
         halo2(1, t).start()
-
-    for t in range(frames):
-        first_level(t)
-
-    for i in range(3):
-        for j in range(3):
-            w2_copy(i, j).wait()
-    for k in (2, 3, 4):
-        plain_copy(k).wait()
 
     def own_copy(t):
         return remote(
@@ -285,19 +276,53 @@
         h3 = h3.astype(BF16).astype(F32)
         res[t] = h3
         mean_square = jnp.mean(h3 * h3, axis=-1, keepdims=True)
-        normed = h3 * lax.rsqrt(mean_square + 1e-06) * gainv[...].astype(F32)
+        normed = h3 * lax.rsqrt(mean_square + 1e-06) * gainv[...].astype(F32).reshape(1, c3)
         keys[t, 0, 0, core] = normed.astype(BF16)
         own_copy(t).start()
 
-        if t > 0:
-            own_copy(t - 1).wait_recv()
-            ring_copy(0, t - 1).start()
-
-    for t in range(frames):
-        second_level(t)
-
-    own_copy(frames - 1).wait_recv()
-    ring_copy(0, frames - 1).start()
+    def take(s, f):
+        block = keys.at[f, s, core]
+        remote(
+            block, block, ring_send.at[lax.rem(s, 2), f], ring_recv.at[s, f], after
+        ).wait_recv()
+
+        if not isinstance(s, int):
+            ring_copy(s - 2, f).wait_send()
+        ring_copy(s, f).start()
+        if not isinstance(s, int):
+
+            @pl.when(s >= 3)
+            def _():
+                pair_copy(s - 2, f).wait_send()
+
+        pair_copy(s, f).start()
+
+    def leave(t):
+        own_copy(t).wait_recv()
+        ring_copy(0, t).start()
+
+    lead = min(2, frames - 1)
+    for t in range(frames + lead):
+        if t < frames:
+            first_level(t)
+        if t == lead:
+            for i in range(3):
+                for j in range(3):
+                    w2_copy(i, j).wait()
+            for k in (2, 3, 4):
+                plain_copy(k).wait()
+        if lead < t < frames:
+            leave(t - lead - 1)
+        if t == frames + lead - 1:
+            take(1, 0)
+        if t >= lead:
+            second_level(t - lead)
+        if t >= max(frames, lead + 1):
+            leave(t - lead - 1)
+    take(1, 1)
+    leave(frames - 1)
+    for f in range(2, frames - 1):
+        take(1, f)
 
     plain_copy(5).wait()
     plain_copy(6).wait()
@@ -308,6 +333,7 @@
     )
     mapped = (mapped * (1.0 / math.sqrt(c3))).astype(BF16)
     qp[...] = mapped.reshape(frames, sites, c3)
+    take(1, frames - 1)
     top[...] = jnp.full(top.shape, -1e30, F32)
     total[...] = jnp.zeros(total.shape, F32)
     mixed[...] = jnp.zeros(mixed.shape, F32)
@@ -329,35 +355,12 @@
 
     def hop(s, carry):
         for f in range(frames):
-            receive_from = remote(
-                keys.at[f, s, core],
-                keys.at[f, s, core],
-                ring_send.at[lax.rem(s, 2), f],
-                ring_recv.at[s, f],
-                after,
-            )
-            receive_from.wait_recv()
-
-            @pl.when(s >= 2)
-            def _():
-                ring_copy(s - 2, f).wait_send()
-
-            ring_copy(s, f).start()
-
-            @pl.when(s >= 3)
-            def _():
-                pair_copy(s - 2, f).wait_send()
-
-            pair_copy(s, f).start()
-
-            @pl.when(s >= 2)
-            def _():
-                pair_copy(s - 1, f).wait_recv()
-                attend(s - 1, f)
-
+            take(s, f)
+            pair_copy(s - 1, f).wait_recv()
+            attend(s - 1, f)
         return carry
 
-    lax.fori_loop(1, hops - 1, hop, 0)
+    lax.fori_loop(2, hops - 1, hop, 0)
 
     end = hops - 1
     for f in range(frames):
@@ -428,7 +431,7 @@
         pltpu.VMEM((3, c2, 3 * c2), BF16),
         pltpu.VMEM((3 * c2, c2), BF16),
         pltpu.VMEM((4 * c2, c3), BF16),
-        pltpu.VMEM((1, c3), BF16),
+        pltpu.VMEM((c3,), BF16),
         pltpu.VMEM((c3, c3), BF16),
         pltpu.VMEM((c3, c3), BF16),
         pltpu.VMEM((c3, c3), BF16),
@@ -478,7 +481,7 @@
         s2,
         t2.reshape(3 * c2, c2),
         r2.reshape(4 * c2, c3),
-        gain.reshape(1, c3),
+        gain,
         wq,
         wk,
         wv,

time: 111 us -> 112 us (level)
  Pallas kernels: 108 us -> 110 us
  local copies, waits for them, and re-layouts: 2.88 us -> 1.62 us
    pallas_call x1, Pallas kernels: 108 us -> 110 us  [per_device(): pl.pallas_call(functools.partial(kernel, n), out_shape=jax.ShapeDtypeStru...]
    reshape x1 -> x0, local copies, waits for them, and re-layouts: 1.26 us -> none  [per_device(): gain.reshape(1, c3)]
where the time goes in v2:
time: 112 us
  Pallas kernels  110 us (98%)
  local copies, waits for them, and re-layouts  1.62 us (1%)
    pallas_call x1, Pallas kernels, per_device(): pl.pallas_call(functools.partial(kernel, n), out_shape=jax.ShapeDtypeStru...  110 us

profile of v2, /device:TPU:37, one launch (start us, length us, event | category | flops | bytes accessed | tf_op | source)
XLA Modules:
  0.0 111.8 jit_solution(1953016542367566561)
XLA Ops:
  0.0 110.2 %encoder.1 = bf16[4,1,48,512]{3,2,1,0:T(8,128)(2,1)} custom-call(bf16[4,4,192,192]{3,2,1,0:T(8,128)(2,1)} %video.1, bf16[3,3,192,128]{3,2,1,0:T(8,128)(2,1)} %s1_.1, bf16[384,128]{1,0:T(8,128)(2,1)} %bitcast.7, bf16[512,256]{1,0:T(8,128)(2,1)} %bitcast.6, bf16[3,3,256,256]{3,2,1,0:T(8,128)(2,1)} %s2_.1, bf16[768,256]{1,0:T(8,128)(2,1)} %bitcast.5, ...), custom_call_target="tpu_custom_call" | custom-call | tf_op jit(solution)/shard_map/encoder/pallas_call | solution.py:466
  110.2 1.6 %copy.14 = bf16[4,1,48,512]{3,2,1,0:T(8,128)(2,1)} copy(bf16[4,1,48,512]{3,2,1,0:T(8,128)(2,1)} %encoder.1) | data formatting | bytes 393216

commit v3 on v2

--- a/solution.py
+++ b/solution.py
@@ -142,9 +142,9 @@
 
     def halo1(d, t):
         if d == 0:
-            src, dst, to = vp.at[t, rows], vp.at[t, 0], down
+            src, dst, to = video.at[t, rows - 1], vp.at[t, 0], down
         else:
-            src, dst, to = vp.at[t, 1], vp.at[t, rows + 1], up
+            src, dst, to = video.at[t, 0], vp.at[t, rows + 1], up
         return remote(src, dst, halo1_send.at[d, t], halo1_recv.at[d, t], to)
 
     def halo2(d, t):
@@ -159,9 +159,10 @@
 
     pl.semaphore_wait(barrier, 4)
     for t in range(frames):
-        video_copy(t).wait()
         halo1(0, t).start()
         halo1(1, t).start()
+    for t in range(frames):
+        video_copy(t).wait()
 
     for i in range(3):
         for j in range(3):
@@ -301,28 +302,18 @@
         own_copy(t).wait_recv()
         ring_copy(0, t).start()
 
-    lead = min(2, frames - 1)
-    for t in range(frames + lead):
-        if t < frames:
-            first_level(t)
-        if t == lead:
-            for i in range(3):
-                for j in range(3):
-                    w2_copy(i, j).wait()
-            for k in (2, 3, 4):
-                plain_copy(k).wait()
-        if lead < t < frames:
-            leave(t - lead - 1)
-        if t == frames + lead - 1:
-            take(1, 0)
-        if t >= lead:
-            second_level(t - lead)
-        if t >= max(frames, lead + 1):
-            leave(t - lead - 1)
-    take(1, 1)
+    for t in range(frames):
+        first_level(t)
+    for i in range(3):
+        for j in range(3):
+            w2_copy(i, j).wait()
+    for k in (2, 3, 4):
+        plain_copy(k).wait()
+    for t in range(frames):
+        second_level(t)
+        if t > 0:
+            leave(t - 1)
     leave(frames - 1)
-    for f in range(2, frames - 1):
-        take(1, f)
 
     plain_copy(5).wait()
     plain_copy(6).wait()
@@ -333,7 +324,8 @@
     )
     mapped = (mapped * (1.0 / math.sqrt(c3))).astype(BF16)
     qp[...] = mapped.reshape(frames, sites, c3)
-    take(1, frames - 1)
+    for f in range(frames):
+        take(1, f)
     top[...] = jnp.full(top.shape, -1e30, F32)
     total[...] = jnp.zeros(total.shape, F32)
     mixed[...] = jnp.zeros(mixed.shape, F32)

time: 112 us -> 110 us (0.982)
  Pallas kernels: 110 us -> 108 us
    pallas_call x1, Pallas kernels: 110 us -> 108 us  [per_device(): pl.pallas_call(functools.partial(kernel, n), out_shape=jax.ShapeDtypeStru...]
where the time goes in v3:
time: 110 us
  Pallas kernels  108 us (98%)
  local copies, waits for them, and re-layouts  1.62 us (1%)
    pallas_call x1, Pallas kernels, per_device(): pl.pallas_call(functools.partial(kernel, n), out_shape=jax.ShapeDtypeStru...  108 us

profile of v3, /device:TPU:37, one launch (start us, length us, event | category | flops | bytes accessed | tf_op | source)
XLA Modules:
  0.0 110.0 jit_solution(587538544252466088)
XLA Ops:
  0.0 108.3 %encoder.1 = bf16[4,1,48,512]{3,2,1,0:T(8,128)(2,1)} custom-call(bf16[4,4,192,192]{3,2,1,0:T(8,128)(2,1)} %video.1, bf16[3,3,192,128]{3,2,1,0:T(8,128)(2,1)} %s1_.1, bf16[384,128]{1,0:T(8,128)(2,1)} %bitcast.7, bf16[512,256]{1,0:T(8,128)(2,1)} %bitcast.6, bf16[3,3,256,256]{3,2,1,0:T(8,128)(2,1)} %s2_.1, bf16[768,256]{1,0:T(8,128)(2,1)} %bitcast.5, ...), custom_call_target="tpu_custom_call" | custom-call | tf_op jit(solution)/shard_map/encoder/pallas_call | solution.py:458
  108.3 1.6 %copy.14 = bf16[4,1,48,512]{3,2,1,0:T(8,128)(2,1)} copy(bf16[4,1,48,512]{3,2,1,0:T(8,128)(2,1)} %encoder.1) | data formatting | bytes 393216

commit v4 on v3

--- a/solution.py
+++ b/solution.py
@@ -368,30 +368,39 @@
         pair_copy(end - 1, f).wait_recv()
         attend(end - 1, f)
 
-    for f in range(frames):
-        @pl.when(core == f // half)
-        def _():
-            ring_copy(end, f).wait_recv()
-            last_copy(f).start()
-
-        pair_copy(end, f).wait_recv()
-        attend(end, f)
+    def finish(group):
+        mean = jnp.concatenate([mixed[f] / total[f][:, :1] for f in group], axis=0)
+        values = jnp.dot(mean.astype(BF16), wvv[...], preferred_element_type=F32).astype(BF16)
+        added = jnp.dot(values, wov[...], preferred_element_type=F32)
+        for k, f in enumerate(group):
+            encoded = res[f] + added[k * sites : (k + 1) * sites]
+            out[f] = encoded.astype(BF16).reshape(out.shape[1:])
 
     for k in (7, 8):
         plain_copy(k).wait()
-    for f in range(frames):
-        @pl.when(core != f // half)
-        def _():
-            last_copy(f).wait_recv()
-
-        attend(0, f)
-
-    mean = jnp.concatenate([mixed[f] / total[f][:, :1] for f in range(frames)], axis=0)
-    values = jnp.dot(mean.astype(BF16), wvv[...], preferred_element_type=F32).astype(BF16)
-    encoded = res[...].reshape(frames * sites, c3) + jnp.dot(
-        values, wov[...], preferred_element_type=F32
-    )
-    out[...] = encoded.astype(BF16).reshape(out.shape)
+    groups = [(k, half + k) for k in range(half)]
+    for k, group in enumerate(groups):
+        for f in range(2 * k, 2 * k + 2):
+            pair_copy(end, f).wait_recv()
+        for f in range(2 * k, 2 * k + 2):
+            attend(end, f)
+        for f in group:
+
+            @pl.when(core == f // half)
+            def _():
+                ring_copy(end, f).wait_recv()
+                last_copy(f).start()
+
+    for group in groups:
+        for f in group:
+
+            @pl.when(core != f // half)
+            def _():
+                last_copy(f).wait_recv()
+
+        for f in group:
+            attend(0, f)
+        finish(group)
 
     for t in range(frames):
         for d in range(2):

time: 110 us -> 110 us (level)
  no operation moved by 1% of the time
where the time goes in v4:
time: 110 us
  Pallas kernels  108 us (98%)
  local copies, waits for them, and re-layouts  1.62 us (1%)
    pallas_call x1, Pallas kernels, per_device(): pl.pallas_call(functools.partial(kernel, n), out_shape=jax.ShapeDtypeStru...  108 us

profile of v4, /device:TPU:37, one launch (start us, length us, event | category | flops | bytes accessed | tf_op | source)
XLA Modules:
  0.0 109.9 jit_solution(16213929520059186301)
XLA Ops:
  0.0 108.3 %encoder.1 = bf16[4,1,48,512]{3,2,1,0:T(8,128)(2,1)} custom-call(bf16[4,4,192,192]{3,2,1,0:T(8,128)(2,1)} %video.1, bf16[3,3,192,128]{3,2,1,0:T(8,128)(2,1)} %s1_.1, bf16[384,128]{1,0:T(8,128)(2,1)} %bitcast.7, bf16[512,256]{1,0:T(8,128)(2,1)} %bitcast.6, bf16[3,3,256,256]{3,2,1,0:T(8,128)(2,1)} %s2_.1, bf16[768,256]{1,0:T(8,128)(2,1)} %bitcast.5, ...), custom_call_target="tpu_custom_call" | custom-call | tf_op jit(solution)/shard_map/encoder/pallas_call | solution.py:467
  108.3 1.6 %copy.14 = bf16[4,1,48,512]{3,2,1,0:T(8,128)(2,1)} copy(bf16[4,1,48,512]{3,2,1,0:T(8,128)(2,1)} %encoder.1) | data formatting | bytes 393216

commit v5 on v4

--- a/solution.py
+++ b/solution.py
@@ -302,17 +302,20 @@
         own_copy(t).wait_recv()
         ring_copy(0, t).start()
 
-    for t in range(frames):
-        first_level(t)
-    for i in range(3):
-        for j in range(3):
-            w2_copy(i, j).wait()
-    for k in (2, 3, 4):
-        plain_copy(k).wait()
-    for t in range(frames):
-        second_level(t)
-        if t > 0:
-            leave(t - 1)
+    lead = min(2, frames - 1)
+    for t in range(frames + lead):
+        if t < frames:
+            first_level(t)
+        if t == lead:
+            for i in range(3):
+                for j in range(3):
+                    w2_copy(i, j).wait()
+            for k in (2, 3, 4):
+                plain_copy(k).wait()
+        if t >= lead:
+            second_level(t - lead)
+        if t > lead:
+            leave(t - lead - 1)
     leave(frames - 1)
 
     plain_copy(5).wait()

time: 110 us -> 112 us (1.018)
  Pallas kernels: 108 us -> 111 us
    pallas_call x1, Pallas kernels: 108 us -> 111 us  [per_device(): pl.pallas_call(functools.partial(kernel, n), out_shape=jax.ShapeDtypeStru...]
where the time goes in v5:
time: 112 us
  Pallas kernels  111 us (99%)
  local copies, waits for them, and re-layouts  1.62 us (1%)
    pallas_call x1, Pallas kernels, per_device(): pl.pallas_call(functools.partial(kernel, n), out_shape=jax.ShapeDtypeStru...  111 us

profile of v5, /device:TPU:37, one launch (start us, length us, event | category | flops | bytes accessed | tf_op | source)
XLA Modules:
  0.0 112.3 jit_solution(2534403356417812716)
XLA Ops:
  0.0 110.7 %encoder.1 = bf16[4,1,48,512]{3,2,1,0:T(8,128)(2,1)} custom-call(bf16[4,4,192,192]{3,2,1,0:T(8,128)(2,1)} %video.1, bf16[3,3,192,128]{3,2,1,0:T(8,128)(2,1)} %s1_.1, bf16[384,128]{1,0:T(8,128)(2,1)} %bitcast.7, bf16[512,256]{1,0:T(8,128)(2,1)} %bitcast.6, bf16[3,3,256,256]{3,2,1,0:T(8,128)(2,1)} %s2_.1, bf16[768,256]{1,0:T(8,128)(2,1)} %bitcast.5, ...), custom_call_target="tpu_custom_call" | custom-call | tf_op jit(solution)/shard_map/encoder/pallas_call | solution.py:470
  110.7 1.6 %copy.14 = bf16[4,1,48,512]{3,2,1,0:T(8,128)(2,1)} copy(bf16[4,1,48,512]{3,2,1,0:T(8,128)(2,1)} %encoder.1) | data formatting | bytes 393216
